TPU v7x, 32 devices: a whole 2x2x4 slice. The times are simulated.
32 devices in a mesh: dp: 4 (over y, core), tensor: 8 (over z, x).
Axes of the slice: x: 2, y: 2, z: 4, core: 2. Of those that a mesh axis runs over, the one named last changes fastest.
Arguments:
- attn_input: bfloat16 [512, 8192], P('dp'), may hold values from -6 to 6
- residual: bfloat16 [512, 8192], P('dp'), may hold values from -3 to 3
- query_weight: bfloat16 [8192, 2048], P('dp', 'tensor'), may hold values from -0.0625 to 0.0625
- query_bias: bfloat16 [2048], P('tensor'), may hold values from -3 to 3
- output_weight: bfloat16 [2048, 8192], P('tensor', 'dp'), may hold values from -0.125 to 0.125
- cached_keys: bfloat16 [4, 8, 1024, 128], P('dp', 'tensor'), may hold values from -305 to 305, as said below
- cached_values: bfloat16 [4, 8, 1024, 128], P('dp', 'tensor'), may hold values from -12 to 12, as said below
- norm_gain: bfloat16 [8192], replicated, may hold values from 0.5 to 1.5
Outputs:
- hidden_out: bfloat16 [512, 8192], P(('dp', 'tensor'))
- normed_out: bfloat16 [512, 8192], P('dp')
Inputs may be any that keep to these rules, and one draw needn't show every extreme that they name: `cached_keys`: groups g and g2 with g // 1 == g2 // 1 carry equal keys. `cached_values`: groups g and g2 with g // 1 == g2 // 1 carry equal values.
All inputs are finite; a program needn't handle non-finite values.
Results may differ from a plain program's by a relative error of at most 0.025.
Values may be sent and summed in bfloat16 or wider, within the bound.
No kernel may reach another device: no remote copies, remote signals or barrier semaphores. Data moves between devices by JAX's collectives and lax.ppermute only.
A program may use at most 64 MiB of HBM per device.

v0:
```python
import jax
import jax.numpy as jnp
from jax import lax
from jax.sharding import PartitionSpec as P

rope_theta = 1000000.0
norm_eps = 1e-06


def rotate(projected, first_pos):
    head_dim = projected.shape[-1]
    half_dim = head_dim // 2
    inv_freq = jnp.power(
        jnp.float32(rope_theta), -2.0 * jnp.arange(half_dim, dtype=jnp.float32) / head_dim
    )
    positions = first_pos + jnp.arange(projected.shape[0], dtype=jnp.float32)
    angles = positions[:, None] * inv_freq[None, :]
    cosine = jnp.cos(angles)[:, None, :]
    sine = jnp.sin(angles)[:, None, :]
    first_half = projected[..., :half_dim]
    second_half = projected[..., half_dim:]
    return jnp.concatenate(
        [first_half * cosine - second_half * sine, second_half * cosine + first_half * sine],
        axis=-1,
    )


def attend(queries, local_keys, local_values):
    count_q = queries.shape[0]
    count_k = local_keys.shape[0]
    scores = jnp.einsum("thd,kd->htk", queries, local_keys, preferred_element_type=jnp.float32) * (
        1.0 / queries.shape[-1] ** 0.5
    )
    visible = jnp.arange(count_k)[None, :] <= (count_k - count_q + jnp.arange(count_q))[:, None]
    scores = jnp.where(visible[None], scores, jnp.float32(-1e30))
    highest = jnp.max(scores, axis=-1, keepdims=True)
    expo = jnp.exp(scores - highest)
    soft = (expo / jnp.sum(expo, axis=-1, keepdims=True)).astype(jnp.bfloat16)
    mixed = jnp.einsum("htk,kd->thd", soft, local_values, preferred_element_type=jnp.float32)
    return mixed.astype(jnp.bfloat16)


def normalize(total, norm_gain):
    mean_square = jnp.mean(total * total, axis=-1, keepdims=True)
    return (total * lax.rsqrt(mean_square + norm_eps) * norm_gain.astype(jnp.float32)).astype(
        jnp.bfloat16
    )


def body(
    attn_input,
    residual,
    query_weight,
    query_bias,
    output_weight,
    cached_keys,
    cached_values,
    norm_gain,
):
    tok_count = attn_input.shape[0]
    ctx_len = cached_keys.shape[2]
    head_dim = cached_keys.shape[3]
    local_heads = query_weight.shape[1] // head_dim
    projected = jnp.dot(
        attn_input,
        lax.all_gather(query_weight, "dp", axis=0, tiled=True),
        preferred_element_type=jnp.float32,
    )
    projected = projected + query_bias.astype(jnp.float32)
    queries = rotate(
        projected.reshape(tok_count, local_heads, head_dim), float(ctx_len - tok_count)
    ).astype(jnp.bfloat16)
    mixed = attend(queries, cached_keys[0, 0], cached_values[0, 0]).reshape(
        tok_count, local_heads * head_dim
    )
    partial_sum = jnp.dot(
        mixed,
        lax.all_gather(output_weight, "dp", axis=1, tiled=True),
        preferred_element_type=jnp.float32,
    )
    own_count = tok_count // lax.axis_size("tensor")
    own_start = lax.axis_index("tensor") * own_count
    summed = lax.psum(partial_sum.astype(jnp.bfloat16), "tensor").astype(jnp.float32)
    total = residual.astype(jnp.float32) + summed
    normed_out = normalize(total, norm_gain)
    hidden_out = lax.dynamic_slice_in_dim(total, own_start, own_count, 0).astype(jnp.bfloat16)
    return (hidden_out, normed_out)


def solution(mesh):
    return jax.shard_map(
        body,
        mesh=mesh,
        in_specs=(
            P("dp", None),
            P("dp", None),
            P("dp", "tensor"),
            P("tensor"),
            P("tensor", "dp"),
            P("dp", "tensor", None, None),
            P("dp", "tensor", None, None),
            P(),
        ),
        out_specs=(P(("dp", "tensor"), None), P("dp", None)),
        check_vma=False,
    )
```

profile of v0, /device:TPU:0, one launch (start us, length us, event | category | flops | bytes accessed | tf_op | source)
XLA Modules:
  0.0 202.9 jit_solution(6312552266347994281)
XLA Ops:
  7.2 0.0 copy-start
  7.2 0.0 all-gather.3.cloned.1.call-start
  7.2 0.7 all-gather.3.cloned.1.call-update
  7.9 0.0 all-gather.5.cloned.1.call-start
  8.0 0.7 all-gather.5.cloned.1.call-update
  8.7 0.0 copy-start.3
  8.7 0.0 all-reduce.2.cloned.1.call-start
  8.7 0.7 convert_element_type.32
  9.4 0.1 iota_compare_fusion
  9.6 0.3 multiply_cosine_fusion
  9.9 36.9 %all-gather.3.cloned.1.call-done = bf16[8192,256]{1,0:T(8,128)(2,1)} async-done(((bf16[2048,256]{1,0:T(8,128)(2,1)}), bf16[8192,256]{1,0:T(8,128)(2,1)}) %all-gather.3.cloned.1.call-update) | async-done | bytes 4194320 | tf_op jit(solution)/shard_map/all_gather | solution.py:66
  46.8 0.0 copy-done
  46.8 2.9 %convolution_add_fusion = f32[128,256]{1,0:T(8,128)S(1)} fusion(bf16[128,8192]{1,0:T(8,128)(2,1)S(1)} %copy-done, bf16[8192,256]{1,0:T(8,128)(2,1)} %all-gather.3.cloned.1.call-done, f32[256]{0:T(256)S(1)} %convert_element_type.32), kind=kOutput, calls=%fused_computation.10 | convolution fusion | flops 536903680 | bytes 6423552 | tf_op jit(solution)/shard_map/dot_general | solution.py:64
  49.7 0.1 reshape.101
  49.7 0.2 fusion.15
  50.0 0.0 copy-start.4
  50.0 0.0 copy-start.5
  50.0 0.6 copy-done.4
  50.6 0.0 copy-done.5
  50.7 0.0 copy-done.3
  50.7 0.6 fusion.16
  51.3 1.2 fusion.4
  52.5 1.7 convolution_convert_fusion.1
  54.2 28.6 %all-gather.5.cloned.1.call-done = bf16[256,8192]{1,0:T(8,128)(2,1)} async-done(((bf16[256,2048]{1,0:T(8,128)(2,1)}), bf16[256,8192]{1,0:T(8,128)(2,1)}) %all-gather.5.cloned.1.call-update) | async-done | bytes 4194320 | tf_op jit(solution)/shard_map/all_gather | solution.py:78
  82.8 0.0 copy-start.6
  82.8 4.3 %convolution_convert_fusion = bf16[128,8192]{1,0:T(8,128)(2,1)} fusion(bf16[128,256]{0,1:T(8,128)(2,1)S(1)} %bitcast.28, bf16[256,8192]{1,0:T(8,128)(2,1)} %all-gather.5.cloned.1.call-done), kind=kOutput, calls=%fused_computation.1 | convolution fusion | flops 537919488 | bytes 6356992 | tf_op jit(solution)/shard_map/dot_general | solution.py:76
  87.1 0.0 all-reduce.2.cloned.1.call-update
  87.1 0.0 copy-done.6
  87.1 102.4 %all-reduce.2.cloned.1.call-done = bf16[128,8192]{1,0:T(8,128)(2,1)} async-done(((bf16[128,8192]{1,0:T(8,128)(2,1)}), bf16[128,8192]{1,0:T(8,128)(2,1)}) %all-reduce.2.cloned.1.call-update) | async-done | bytes 2097168 | tf_op jit(solution)/shard_map/psum | solution.py:83
  189.6 0.0 copy-start.1
  189.6 0.0 copy-start.2
  189.6 3.1 %multiply_reduce_fusion = f32[128]{0:T(128)S(1)} fusion(bf16[128,8192]{1,0:T(8,128)(2,1)} %all-reduce.2.cloned.1.call-done, bf16[128,8192]{1,0:T(8,128)(2,1)} %param.9), kind=kLoop, calls=%fused_computation.3 | loop fusion | flops 5242752 | bytes 4194816 | tf_op jit(solution)/shard_map/reduce_sum | solution.py:44
  192.7 0.0 copy-done.1
  192.7 0.3 copy-done.2
  193.0 0.5 convert_add_fusion
  193.5 0.7 dynamic-slice_convert_fusion
  194.3 2.1 %multiply_convert_fusion = bf16[128,8192]{1,0:T(8,128)(2,1)} fusion(f32[8192]{0:T(1024)S(1)} %convert_element_type.39, f32[128]{0:T(128)S(1)} %add_rsqrt_fusion, bf16[128,8192]{1,0:T(8,128)(2,1)S(1)} %copy-done.2, bf16[128,8192]{1,0:T(8,128)(2,1)S(1)} %copy-done.1), kind=kLoop, calls=%fused_computation.2 | loop fusion | flops 6291456 | bytes 6324736 | tf_op jit(solution)/shard_map/convert_element_type | solution.py:45
  (6 shorter events, 0.1 us)
Async XLA Ops:
  7.2 39.6 %copy-start = (bf16[128,8192]{1,0:T(8,128)(2,1)S(1)}, bf16[128,8192]{1,0:T(8,128)(2,1)}, u32[]{:S(2)}) copy-start(bf16[128,8192]{1,0:T(8,128)(2,1)} %param.8) | copy-start | bytes 6291460
  7.2 39.6 %all-gather.3.cloned.1.call-start = ((), (), s32[]{:S(2)}) async-start(), calls=%async_computation | async-start | bytes 5242880 | tf_op jit(solution)/shard_map/all_gather | solution.py:66
  7.9 74.9 %all-gather.5.cloned.1.call-start = ((), (), s32[]{:S(2)}) async-start(), calls=%async_computation.1 | async-start | bytes 5242880 | tf_op jit(solution)/shard_map/all_gather | solution.py:78
  8.7 42.0 %copy-start.3 = (bf16[1,1,1024,128]{3,2,1,0:T(8,128)(2,1)S(1)}, bf16[1,1,1024,128]{3,2,1,0:T(8,128)(2,1)}, u32[]{:S(2)}) copy-start(bf16[1,1,1024,128]{3,2,1,0:T(8,128)(2,1)} %param.13) | copy-start | bytes 786436
  8.7 180.9 %all-reduce.2.cloned.1.call-start = ((), (), s32[]{:S(2)}) async-start(), calls=%async_computation.2 | async-start | bytes 4194304 | tf_op jit(solution)/shard_map/psum | solution.py:83
  50.0 0.6 copy-start.4
  50.0 0.6 copy-start.5
  82.8 4.3 %copy-start.6 = (bf16[8192]{0:T(1024)(128)(2,1)S(1)}, bf16[8192]{0:T(1024)(128)(2,1)}, u32[]{:S(2)}) copy-start(bf16[8192]{0:T(1024)(128)(2,1)} %param.15) | copy-start | bytes 49156
  189.6 3.2 %copy-start.1 = (bf16[128,8192]{1,0:T(8,128)(2,1)S(1)}, bf16[128,8192]{1,0:T(8,128)(2,1)}, u32[]{:S(2)}) copy-start(bf16[128,8192]{1,0:T(8,128)(2,1)} %param.9) | copy-start | bytes 6291460
  189.6 3.5 %copy-start.2 = (bf16[128,8192]{1,0:T(8,128)(2,1)S(1)}, bf16[128,8192]{1,0:T(8,128)(2,1)}, u32[]{:S(2)}) copy-start(bf16[128,8192]{1,0:T(8,128)(2,1)} %all-reduce.2.cloned.1.call-done) | copy-start | bytes 6291460
Sparse Core Ops, SparseCore 0:
  9.5 37.1 all-gather.2
  48.3 34.4 all-gather.4
  87.2 102.2 all-reduce.1
where the time goes:
time: 203 us
  waiting for transfers between devices  169 us (83%)
  between operations  13.9 us (7%)
  matrix products  10.7 us (5%)
  other arithmetic  6.93 us (3%)
    psum x1, waiting for transfers between devices, body(): lax.psum(partial_sum.astype(jnp.bfloat16), 'tensor').astype(jnp.float32)  102 us
    all_gather x1, waiting for transfers between devices, body(): lax.all_gather(query_weight, 'dp', axis=0, tiled=True)  36.9 us
    all_gather x1, waiting for transfers between devices, body(): lax.all_gather(output_weight, 'dp', axis=1, tiled=True)  28.6 us
    dot_general x1, matrix products, body(): jnp.dot(mixed, lax.all_gather(output_weight, 'dp', axis=1, tiled=True), p...  4.27 us
  transfers between devices with their start and end apart: 3, of which 3 were waited for; matrix products, arithmetic and copies ran while one was open for 4% of the time, Pallas kernels for 0%

commit v1 on v0

--- a/solution.py
+++ b/solution.py
@@ -75,7 +75,7 @@
     )
     partial_sum = jnp.dot(
         mixed,
-        lax.all_gather(output_weight, "dp", axis=1, tiled=True),
+        jnp.concatenate(lax.all_gather(output_weight, "dp"), axis=1),
         preferred_element_type=jnp.float32,
     )
     own_count = tok_count // lax.axis_size("tensor")

time: 203 us -> 211 us (1.039)
  local copies, waits for them, and re-layouts: 1.98 us -> 8.27 us
    reshape x0 -> x1, local copies, waits for them, and re-layouts: none -> 6.29 us  [body(): jnp.concatenate(lax.all_gather(output_weight, 'dp'), axis=1)]
  transfers between devices with their start and end apart: 3 -> 3, of which waited for: 3 -> 3; matrix products, arithmetic and copies ran while one was open for 4% -> 3% of each run, Pallas kernels for 0% -> 0%
where the time goes in v1:
time: 211 us
  waiting for transfers between devices  171 us (81%)
  between operations  13.9 us (7%)
  matrix products  10.5 us (5%)
  local copies, waits for them, and re-layouts  8.27 us (4%)
  other arithmetic  6.93 us (3%)
    psum x1, waiting for transfers between devices, body(): lax.psum(partial_sum.astype(jnp.bfloat16), 'tensor').astype(jnp.float32)  102 us
    all_gather x1, waiting for transfers between devices, body(): lax.all_gather(query_weight, 'dp', axis=0, tiled=True)  36.9 us
    all_gather x1, waiting for transfers between devices, body(): lax.all_gather(output_weight, 'dp')  30.3 us
    reshape x1, local copies, waits for them, and re-layouts, body(): jnp.concatenate(lax.all_gather(output_weight, 'dp'), axis=1)  6.29 us
    dot_general x1, matrix products, body(): jnp.dot(mixed, jnp.concatenate(lax.all_gather(output_weight, 'dp'), axis=...  5.01 us
  transfers between devices with their start and end apart: 3, of which 3 were waited for; matrix products, arithmetic and copies ran while one was open for 3% of the time, Pallas kernels for 0%

profile of v1, /device:TPU:0, one launch (start us, length us, event | category | flops | bytes accessed | tf_op | source)
XLA Modules:
  0.0 210.6 jit_solution(11857248919753665595)
XLA Ops:
  7.2 0.0 copy-start
  7.2 0.0 all-gather.4.cloned.1.call-start
  7.2 0.7 all-gather.4.cloned.1.call-update
  7.9 0.0 all-gather.6.cloned.1.call-start
  8.0 0.7 all-gather.6.cloned.1.call-update
  8.7 0.0 copy-start.3
  8.7 0.0 all-reduce.2.cloned.1.call-start
  8.7 0.7 convert_element_type.32
  9.4 0.1 iota_compare_fusion
  9.6 0.3 multiply_cosine_fusion
  9.9 36.9 %all-gather.4.cloned.1.call-done = bf16[8192,256]{1,0:T(8,128)(2,1)} async-done(((bf16[2048,256]{1,0:T(8,128)(2,1)}), bf16[8192,256]{1,0:T(8,128)(2,1)}) %all-gather.4.cloned.1.call-update) | async-done | bytes 4194320 | tf_op jit(solution)/shard_map/all_gather | solution.py:66
  46.8 0.0 copy-done
  46.8 2.9 %convolution_add_fusion = f32[128,256]{1,0:T(8,128)S(1)} fusion(bf16[128,8192]{1,0:T(8,128)(2,1)S(1)} %copy-done, bf16[8192,256]{1,0:T(8,128)(2,1)} %all-gather.4.cloned.1.call-done, f32[256]{0:T(256)S(1)} %convert_element_type.32), kind=kOutput, calls=%fused_computation.10 | convolution fusion | flops 536903680 | bytes 6423552 | tf_op jit(solution)/shard_map/dot_general | solution.py:64
  49.7 0.1 reshape.107
  49.7 0.2 fusion.15
  50.0 0.0 copy-start.4
  50.0 0.0 copy-start.5
  50.0 0.6 copy-done.4
  50.6 0.0 copy-done.5
  50.7 0.0 copy-done.3
  50.7 0.6 fusion.16
  51.3 1.2 fusion.4
  52.5 30.3 %all-gather.6.cloned.1.call-done = bf16[1024,2048]{1,0:T(8,128)(2,1)} async-done(((bf16[256,2048]{1,0:T(8,128)(2,1)}), bf16[1024,2048]{1,0:T(8,128)(2,1)}) %all-gather.6.cloned.1.call-update) | async-done | bytes 4194320 | tf_op jit(solution)/shard_map/all_gather | solution.py:78
  82.8 0.0 copy-start.7
  82.8 6.3 %copy.19 = bf16[256,4,2048]{0,2,1:T(8,128)(2,1)} copy(bf16[256,4,2048]{2,0,1:T(8,128)(2,1)} %bitcast.33) | data formatting | bytes 8388608 | tf_op jit(solution)/shard_map/reshape | solution.py:78
  89.1 0.0 copy-done.7
  89.1 0.7 convolution_convert_fusion.1
  89.8 0.0 copy-start.6
  89.8 5.0 %convolution_convert_fusion = bf16[128,8192]{1,0:T(8,128)(2,1)} fusion(bf16[128,256]{0,1:T(8,128)(2,1)S(1)} %bitcast.34, bf16[256,8192]{0,1:T(8,128)(2,1)} %bitcast.32), kind=kOutput, calls=%fused_computation.1 | convolution fusion | flops 537919488 | bytes 6356992 | tf_op jit(solution)/shard_map/dot_general | solution.py:76
  94.8 0.0 all-reduce.2.cloned.1.call-update
  94.9 0.0 copy-done.6
  94.9 102.4 %all-reduce.2.cloned.1.call-done = bf16[128,8192]{1,0:T(8,128)(2,1)} async-done(((bf16[128,8192]{1,0:T(8,128)(2,1)}), bf16[128,8192]{1,0:T(8,128)(2,1)}) %all-reduce.2.cloned.1.call-update) | async-done | bytes 2097168 | tf_op jit(solution)/shard_map/psum | solution.py:83
  197.3 0.0 copy-start.1
  197.3 0.0 copy-start.2
  197.3 3.1 %multiply_reduce_fusion = f32[128]{0:T(128)S(1)} fusion(bf16[128,8192]{1,0:T(8,128)(2,1)} %all-reduce.2.cloned.1.call-done, bf16[128,8192]{1,0:T(8,128)(2,1)} %param.9), kind=kLoop, calls=%fused_computation.3 | loop fusion | flops 5242752 | bytes 4194816 | tf_op jit(solution)/shard_map/reduce_sum | solution.py:44
  200.4 0.0 copy-done.1
  200.5 0.3 copy-done.2
  200.8 0.5 convert_add_fusion
  201.3 0.7 dynamic-slice_convert_fusion
  202.0 2.1 multiply_convert_fusion
  (6 shorter events, 0.1 us)
Async XLA Ops:
  7.2 39.6 %copy-start = (bf16[128,8192]{1,0:T(8,128)(2,1)S(1)}, bf16[128,8192]{1,0:T(8,128)(2,1)}, u32[]{:S(2)}) copy-start(bf16[128,8192]{1,0:T(8,128)(2,1)} %param.8) | copy-start | bytes 6291460
  7.2 39.6 %all-gather.4.cloned.1.call-start = ((), (), s32[]{:S(2)}) async-start(), calls=%async_computation | async-start | bytes 5242880 | tf_op jit(solution)/shard_map/all_gather | solution.py:66
  7.9 74.9 %all-gather.6.cloned.1.call-start = ((), (), s32[]{:S(2)}) async-start(), calls=%async_computation.2 | async-start | bytes 5242880 | tf_op jit(solution)/shard_map/all_gather | solution.py:78
  8.7 42.0 %copy-start.3 = (bf16[1,1,1024,128]{3,2,1,0:T(8,128)(2,1)S(1)}, bf16[1,1,1024,128]{3,2,1,0:T(8,128)(2,1)}, u32[]{:S(2)}) copy-start(bf16[1,1,1024,128]{3,2,1,0:T(8,128)(2,1)} %param.13) | copy-start | bytes 786436
  8.7 188.6 %all-reduce.2.cloned.1.call-start = ((), (), s32[]{:S(2)}) async-start(), calls=%async_computation.1 | async-start | bytes 4194304 | tf_op jit(solution)/shard_map/psum | solution.py:83
  50.0 0.6 copy-start.4
  50.0 0.6 copy-start.5
  82.8 6.3 %copy-start.7 = (bf16[1,1,1024,128]{3,2,1,0:T(8,128)(2,1)S(1)}, bf16[1,1,1024,128]{3,2,1,0:T(8,128)(2,1)}, u32[]{:S(2)}) copy-start(bf16[1,1,1024,128]{3,2,1,0:T(8,128)(2,1)} %param.14) | copy-start | bytes 786436
  89.8 5.1 %copy-start.6 = (bf16[8192]{0:T(1024)(128)(2,1)S(1)}, bf16[8192]{0:T(1024)(128)(2,1)}, u32[]{:S(2)}) copy-start(bf16[8192]{0:T(1024)(128)(2,1)} %param.15) | copy-start | bytes 49156
  197.3 3.2 %copy-start.1 = (bf16[128,8192]{1,0:T(8,128)(2,1)S(1)}, bf16[128,8192]{1,0:T(8,128)(2,1)}, u32[]{:S(2)}) copy-start(bf16[128,8192]{1,0:T(8,128)(2,1)} %param.9) | copy-start | bytes 6291460
  197.3 3.5 %copy-start.2 = (bf16[128,8192]{1,0:T(8,128)(2,1)S(1)}, bf16[128,8192]{1,0:T(8,128)(2,1)}, u32[]{:S(2)}) copy-start(bf16[128,8192]{1,0:T(8,128)(2,1)} %all-reduce.2.cloned.1.call-done) | copy-start | bytes 6291460
Sparse Core Ops, SparseCore 0:
  9.5 37.1 all-gather.3
  48.3 34.4 all-gather.5
  95.0 102.2 all-reduce.1

commit v2 on v0

--- a/solution.py
+++ b/solution.py
@@ -80,7 +80,9 @@
     )
     own_count = tok_count // lax.axis_size("tensor")
     own_start = lax.axis_index("tensor") * own_count
-    summed = lax.psum(partial_sum.astype(jnp.bfloat16), "tensor").astype(jnp.float32)
+    summed = jnp.sum(lax.all_gather(partial_sum.astype(jnp.bfloat16), "tensor"), axis=0).astype(
+        jnp.float32
+    )
     total = residual.astype(jnp.float32) + summed
     normed_out = normalize(total, norm_gain)
     hidden_out = lax.dynamic_slice_in_dim(total, own_start, own_count, 0).astype(jnp.bfloat16)

time: 203 us -> 339 us (1.67)
  waiting for transfers between devices: 169 us -> 294 us
  other arithmetic: 6.93 us -> 17.4 us
    all_gather x0 -> x1, waiting for transfers between devices: none -> 227 us  [body(): lax.all_gather(partial_sum.astype(jnp.bfloat16), 'tensor')]
    psum x1 -> x0, waiting for transfers between devices: 102 us -> none  [body(): lax.psum(partial_sum.astype(jnp.bfloat16), 'tensor').astype(jnp.float32)]
    reduce_sum x0 -> x1, other arithmetic: none -> 10.5 us  [body(): jnp.sum(lax.all_gather(partial_sum.astype(jnp.bfloat16), 'tensor'), axis=0)]
  transfers between devices with their start and end apart: 3 -> 3, of which waited for: 3 -> 3; matrix products, arithmetic and copies ran while one was open for 4% -> 2% of each run, Pallas kernels for 0% -> 0%
where the time goes in v2:
time: 339 us; the launch traced here: 338 us
  waiting for transfers between devices  294 us (87%)
  other arithmetic  17.4 us (5%)
  between operations  13.9 us (4%)
  matrix products  10.7 us (3%)
    all_gather x1, waiting for transfers between devices, body(): lax.all_gather(partial_sum.astype(jnp.bfloat16), 'tensor')  227 us
    all_gather x1, waiting for transfers between devices, body(): lax.all_gather(query_weight, 'dp', axis=0, tiled=True)  36.9 us
    all_gather x1, waiting for transfers between devices, body(): lax.all_gather(output_weight, 'dp', axis=1, tiled=True)  28.6 us
    reduce_sum x1, other arithmetic, body(): jnp.sum(lax.all_gather(partial_sum.astype(jnp.bfloat16), 'tensor'), axis=0)  10.5 us
  transfers between devices with their start and end apart: 3, of which 3 were waited for; matrix products, arithmetic and copies ran while one was open for 2% of the time, Pallas kernels for 0%

profile of v2, /device:TPU:0, one launch (start us, length us, event | category | flops | bytes accessed | tf_op | source)
XLA Modules:
  0.0 338.3 jit_solution(11752251626231080506)
XLA Ops:
  7.2 0.0 copy-start
  7.2 0.0 all-gather.5.cloned.1.call-start
  7.2 0.7 all-gather.5.cloned.1.call-update
  7.9 0.0 all-gather.7.cloned.1.call-start
  8.0 0.7 all-gather.7.cloned.1.call-update
  8.7 0.0 copy-start.3
  8.7 0.0 all-gather.9.cloned.1.call-start
  8.7 0.7 convert_element_type.34
  9.4 0.1 iota_compare_fusion
  9.6 0.3 multiply_cosine_fusion
  9.9 36.9 %all-gather.5.cloned.1.call-done = bf16[8192,256]{1,0:T(8,128)(2,1)} async-done(((bf16[2048,256]{1,0:T(8,128)(2,1)}), bf16[8192,256]{1,0:T(8,128)(2,1)}) %all-gather.5.cloned.1.call-update) | async-done | bytes 4194320 | tf_op jit(solution)/shard_map/all_gather | solution.py:66
  46.8 0.0 copy-done
  46.8 2.9 convolution_add_fusion
  49.7 0.1 reshape.101
  49.7 0.2 fusion.15
  50.0 0.0 copy-start.4
  50.0 0.0 copy-start.5
  50.0 0.6 copy-done.4
  50.6 0.0 copy-done.5
  50.7 0.0 copy-done.3
  50.7 0.6 fusion.16
  51.3 1.2 fusion.4
  52.5 1.7 convolution_convert_fusion.1
  54.2 28.6 %all-gather.7.cloned.1.call-done = bf16[256,8192]{1,0:T(8,128)(2,1)} async-done(((bf16[256,2048]{1,0:T(8,128)(2,1)}), bf16[256,8192]{1,0:T(8,128)(2,1)}) %all-gather.7.cloned.1.call-update) | async-done | bytes 4194320 | tf_op jit(solution)/shard_map/all_gather | solution.py:78
  82.8 0.0 copy-start.6
  82.8 4.3 %convolution_convert_fusion = bf16[128,8192]{1,0:T(8,128)(2,1)} fusion(bf16[128,256]{0,1:T(8,128)(2,1)S(1)} %bitcast.30, bf16[256,8192]{1,0:T(8,128)(2,1)} %all-gather.7.cloned.1.call-done), kind=kOutput, calls=%fused_computation.1 | convolution fusion | flops 537919488 | bytes 6356992 | tf_op jit(solution)/shard_map/dot_general | solution.py:76
  87.1 0.0 all-gather.9.cloned.1.call-update
  87.1 0.0 copy-done.6
  87.1 227.4 %all-gather.9.cloned.1.call-done = bf16[1024,8192]{1,0:T(8,128)(2,1)} async-done(((bf16[128,8192]{1,0:T(8,128)(2,1)}), bf16[1024,8192]{1,0:T(8,128)(2,1)}) %all-gather.9.cloned.1.call-update) | async-done | bytes 16777232 | tf_op jit(solution)/shard_map/all_gather | solution.py:83
  314.5 10.5 %reduce_sum.31 = bf16[128,8192]{1,0:T(8,128)(2,1)} reduce(bf16[8,128,8192]{2,1,0:T(8,128)(2,1)} %bitcast.29, bf16[]{:T(256)} %constant.12.clone.1), dimensions={0}, to_apply=%region_2.3 | reduce | flops 7340032 | bytes 18874370 | tf_op jit(solution)/shard_map/reduce_sum | solution.py:83
  325.0 0.0 copy-start.1
  325.0 0.0 copy-start.2
  325.0 3.1 multiply_reduce_fusion
  328.1 0.0 copy-done.1
  328.2 0.3 copy-done.2
  328.5 0.5 convert_add_fusion
  329.0 2.1 multiply_convert_fusion
  331.1 0.7 dynamic-slice_convert_fusion
  (6 shorter events, 0.1 us)
Async XLA Ops:
  7.2 39.6 %copy-start = (bf16[128,8192]{1,0:T(8,128)(2,1)S(1)}, bf16[128,8192]{1,0:T(8,128)(2,1)}, u32[]{:S(2)}) copy-start(bf16[128,8192]{1,0:T(8,128)(2,1)} %param.8) | copy-start | bytes 6291460
  7.2 39.6 %all-gather.5.cloned.1.call-start = ((), (), s32[]{:S(2)}) async-start(), calls=%async_computation | async-start | bytes 5242880 | tf_op jit(solution)/shard_map/all_gather | solution.py:66
  7.9 74.9 %all-gather.7.cloned.1.call-start = ((), (), s32[]{:S(2)}) async-start(), calls=%async_computation.1 | async-start | bytes 5242880 | tf_op jit(solution)/shard_map/all_gather | solution.py:78
  8.7 42.0 %copy-start.3 = (bf16[1,1,1024,128]{3,2,1,0:T(8,128)(2,1)S(1)}, bf16[1,1,1024,128]{3,2,1,0:T(8,128)(2,1)}, u32[]{:S(2)}) copy-start(bf16[1,1,1024,128]{3,2,1,0:T(8,128)(2,1)} %param.13) | copy-start | bytes 786436
  8.7 305.9 %all-gather.9.cloned.1.call-start = ((), (), s32[]{:S(2)}) async-start(), calls=%async_computation.2 | async-start | bytes 18874368 | tf_op jit(solution)/shard_map/all_gather | solution.py:83
  50.0 0.6 copy-start.4
  50.0 0.6 copy-start.5
  82.8 4.3 %copy-start.6 = (bf16[8192]{0:T(1024)(128)(2,1)S(1)}, bf16[8192]{0:T(1024)(128)(2,1)}, u32[]{:S(2)}) copy-start(bf16[8192]{0:T(1024)(128)(2,1)} %param.15) | copy-start | bytes 49156
  325.0 3.1 copy-start.1
  325.0 3.5 %copy-start.2 = (bf16[128,8192]{1,0:T(8,128)(2,1)S(1)}, bf16[128,8192]{1,0:T(8,128)(2,1)}, u32[]{:S(2)}) copy-start(bf16[128,8192]{1,0:T(8,128)(2,1)} %param.9) | copy-start | bytes 6291460
Sparse Core Ops, SparseCore 0:
  9.5 37.1 all-gather.4
  48.3 34.4 all-gather.6
  87.2 227.2 all-gather.8
